TPU v7x, 32 devices: a whole 2x2x4 slice. The times are simulated.
32 devices in a mesh: tm: 8 (over y, x, core), chan: 4 (over z).
Axes of the slice: x: 2, y: 2, z: 4, core: 2. Of those that a mesh axis runs over, the one named last changes fastest.
Arguments:
- auxiliary: float32 [512, 262144], P('chan', 'tm'), may hold values from -30 to 30
- proofs: float32 [64, 262144], P('chan', 'tm'), may hold values from -12 to 12
Outputs:
- coherence: float32 [512, 64, 4096], P('chan', None, 'tm')
All inputs are finite; a program needn't handle non-finite values.
Results may differ from a plain program's by a relative error of at most 0.00076.
Values may be sent and summed in bfloat16 or wider, within the bound.
A program may use at most 192 MiB of HBM per device.

v0:
```python
import math

import jax
import jax.numpy as jnp
from jax import lax
from jax.sharding import PartitionSpec as P

SEG_LEN = 8192
FACTOR = 64
STRIDE = 4096
BINS = 4096


def shifted(value, axis, by):
    peers = lax.axis_size(axis)
    pairs = [(i, i + by) for i in range(peers) if 0 <= i + by < peers]
    return lax.ppermute(value, axis, pairs)


def angle_table(left_count, right_count, modulus):
    left_index = jnp.arange(left_count, dtype=jnp.int32)
    right_index = jnp.arange(right_count, dtype=jnp.int32)
    product = left_index[:, None] * right_index[None, :] % modulus
    return 2.0 * math.pi / modulus * product.astype(jnp.float32)


def transform_block(windowed):
    row_count = windowed.shape[0]
    second = SEG_LEN // FACTOR
    highest = lax.Precision.HIGHEST
    angle_first = angle_table(FACTOR, FACTOR, FACTOR)
    angle_twist = angle_table(FACTOR, second, SEG_LEN)
    angle_second = angle_table(second, second // 2, second)
    cos_twist = jnp.cos(angle_twist)
    sin_twist = jnp.sin(angle_twist)
    cos_second = jnp.cos(angle_second)
    sin_second = jnp.sin(angle_second)
    shaped = windowed.reshape(row_count, FACTOR, second)
    real_one = jnp.einsum("rpq,pk->rkq", shaped, jnp.cos(angle_first), precision=highest)
    imag_one = -jnp.einsum("rpq,pk->rkq", shaped, jnp.sin(angle_first), precision=highest)
    real_two = real_one * cos_twist + imag_one * sin_twist
    imag_two = imag_one * cos_twist - real_one * sin_twist
    real_out = jnp.einsum("rkq,qm->rmk", real_two, cos_second, precision=highest) + jnp.einsum(
        "rkq,qm->rmk", imag_two, sin_second, precision=highest
    )
    imag_out = jnp.einsum("rkq,qm->rmk", imag_two, cos_second, precision=highest) - jnp.einsum(
        "rkq,qm->rmk", real_two, sin_second, precision=highest
    )
    return (real_out.reshape(row_count, BINS), imag_out.reshape(row_count, BINS))


def transform(windowed):
    row_count = windowed.shape[0]
    block_rows = math.gcd(row_count, 64)
    blocks = windowed.reshape(row_count // block_rows, block_rows, SEG_LEN)
    real_out, imag_out = lax.map(transform_block, blocks)
    return (real_out.reshape(row_count, BINS), imag_out.reshape(row_count, BINS))


def segments_of(signal, seg_count):
    channels = signal.shape[0]
    blocks = signal.reshape(channels, seg_count + 1, STRIDE)
    segments = jnp.concatenate([blocks[:, :-1], blocks[:, 1:]], axis=2)
    position = jnp.arange(SEG_LEN, dtype=jnp.float32)
    window = 0.5 - 0.5 * jnp.cos(2.0 * math.pi * position / SEG_LEN)
    return (segments * window).reshape(channels * seg_count, SEG_LEN)


def channel_totals(local_sums):
    return lax.psum((local_sums[0], local_sums[1]), "tm")


def coherence_block(aux_moved, aux_power, wit_piece):
    left_real = jnp.concatenate([aux_moved[0], aux_moved[1]], axis=1)
    left_imag = jnp.concatenate([aux_moved[1], -aux_moved[0]], axis=1)
    right_side = jnp.concatenate([wit_piece[0], wit_piece[1]], axis=1)
    cross_real = jnp.einsum(
        "csf,wsf->cwf", left_real, right_side, preferred_element_type=jnp.float32
    )
    cross_imag = jnp.einsum(
        "csf,wsf->cwf", left_imag, right_side, preferred_element_type=jnp.float32
    )
    wit_float = wit_piece.astype(jnp.float32)
    wit_power = jnp.sum(wit_float * wit_float, axis=(0, 2))
    return (cross_real * cross_real + cross_imag * cross_imag) / (
        (aux_power[:, None, :] + 1e-06) * (wit_power[None, :, :] + 1e-06)
    )


def per_device(auxiliary, proofs):
    aux_rows = auxiliary.shape[0]
    seg_count = auxiliary.shape[1] // STRIDE
    tm_size = lax.axis_size("tm")
    next_aux, next_wit = shifted((auxiliary[:, :STRIDE], proofs[:, :STRIDE]), "tm", -1)
    signal = jnp.concatenate(
        [
            jnp.concatenate([auxiliary, next_aux], axis=1),
            jnp.concatenate([proofs, next_wit], axis=1),
        ],
        axis=0,
    )
    channels = signal.shape[0]
    local_sums = (jnp.sum(auxiliary, axis=1), jnp.sum(proofs, axis=1))
    total_samples = auxiliary.shape[1] * tm_size
    real_part, imag_part = transform(segments_of(signal, seg_count))
    totals = channel_totals(local_sums)
    channel_means = jnp.concatenate(totals) / total_samples
    bin_index = jnp.arange(BINS, dtype=jnp.int32)
    offset_table = jnp.where(
        bin_index == 0, -0.5 * SEG_LEN, jnp.where(bin_index == 1, 0.25 * SEG_LEN, 0.0)
    ).astype(jnp.float32)
    real_part = real_part + jnp.repeat(channel_means, seg_count)[:, None] * offset_table[None, :]
    spectra = (
        jnp.stack([real_part, imag_part]).astype(jnp.bfloat16).reshape(2, channels, seg_count, BINS)
    )
    aux_spec = spectra[:, :aux_rows]
    wit_spec = spectra[:, aux_rows:]
    aux_moved, wit_moved = (
        lax.all_to_all(aux_spec, "tm", split_axis=3, concat_axis=2, tiled=True),
        lax.all_to_all(wit_spec, "tm", split_axis=3, concat_axis=2, tiled=True),
    )
    kept_segments = seg_count * tm_size - 1
    aux_moved = aux_moved[:, :, :kept_segments]
    wit_moved = wit_moved[:, :, :kept_segments]
    aux_float = aux_moved.astype(jnp.float32)
    aux_power = jnp.sum(aux_float * aux_float, axis=(0, 2))
    return coherence_block(
        aux_moved, aux_power, lax.all_gather(wit_moved, "chan", axis=1, tiled=True)
    )


def solution(mesh):
    return jax.shard_map(
        per_device,
        mesh=mesh,
        in_specs=(P("chan", "tm"), P("chan", "tm")),
        out_specs=P("chan", None, "tm"),
        check_vma=False,
    )
```

profile of v0, /device:TPU:0, one launch (start us, length us, event | category | flops | bytes accessed | tf_op | source)
XLA Modules:
  0.0 1519.9 jit_solution(11121710718804022927)
XLA Ops:
  11.1 6.6 reduce_sum.36
  19.4 28.3 %all-reduce = (f32[16]{0:T(128)S(1)}, f32[128]{0:T(128)S(1)}) all-reduce(f32[16]{0:T(128)S(1)} %reduce_sum.37, f32[128]{0:T(128)S(1)} %reduce_sum.36), channel_id=1, replica_groups=mesh['tm'=8,'chan'=4] {'tm'}, use_global_device_ids=true, to_apply=%region_5.6 | all-reduce | flops 144 | bytes 1152 | tf_op jit(solution)/shard_map/psum | solution.py:70
  47.8 19.2 %maximum_maximum_fusion = f32[144,36864]{1,0:T(8,128)} fusion(f32[16,4096]{1,0:T(8,128)S(1)} %collective-permute-done.1, f32[16,32768]{1,0:T(8,128)S(1)} %copy-done.6, f32[128,4096]{1,0:T(8,128)} %collective-permute-done, f32[128,32768]{1,0:T(8,128)} %param.4), kind=kLoop, calls=%fused_computation.83 | loop fusion | flops 15925248 | bytes 42467328 | tf_op jit(solution)/shard_map/concatenate | solution.py:95
  67.0 23.5 %reshape.121 = f32[144,9,4096]{2,1,0:T(8,128)} reshape(f32[144,36864]{1,0:T(8,128)} %maximum_maximum_fusion) | data formatting | bytes 42467328 | tf_op jit(solution)/shard_map/reshape | solution.py:62
  90.5 32.4 %fusion.86 = (f32[144,8,4096]{2,1,0:T(8,128)}, f32[144,8,4096]{2,1,0:T(8,128)}) fusion(f32[144,9,4096]{2,1,0:T(8,128)} %reshape.121), kind=kLoop, calls=%fused_computation.109 | loop fusion | bytes 75497472 | tf_op jit(solution)/shard_map/slice | solution.py:63
  122.9 24.7 %maximum_multiply_fusion = f32[18,64,8192]{2,1,0:T(8,128)} fusion(f32[18,64,4096]{2,1,0:T(8,128)} %bitcast.103, f32[18,64,4096]{2,1,0:T(8,128)} %bitcast.102, f32[8192]{0:T(1024)S(1)} %multiply_subtract_fusion.3), kind=kLoop, calls=%fused_computation.80 | loop fusion | flops 18874368 | bytes 75530240 | tf_op jit(solution)/shard_map/mul | solution.py:66
  147.7 764.7 %while.15 = (s32[]{:T(128)}, f32[18,64,4096]{2,1,0:T(8,128)}, bf16[18,64,4096]{2,1,0:T(8,128)(2,1)}, f32[18,64,8192]{2,1,0:T(8,128)}, s32[]{:T(128)}) while((s32[]{:T(128)}, f32[18,64,4096]{2,1,0:T(8,128)}, bf16[18,64,4096]{2,1,0:T(8,128)(2,1)}, f32[18,64,8192]{2,1,0:T(8,128)}, s32[]{:T(128)}) %tuple.35), condition=%wide.region_1.0_spmd, body=%wide.region_0.0_spmd.sunk | while | flops 2425782272 | bytes 56426632 | solution.py:56
  182.6 7.8 fusion.122
  190.4 9.2 add_bitcast_fusion.2
  224.2 7.8 fusion.122
  232.0 9.2 add_bitcast_fusion.2
  265.8 7.8 fusion.122
  273.6 9.2 add_bitcast_fusion.2
  299.6 6.3 subtract_bitcast_fusion.2
  307.5 7.8 fusion.122
  315.3 9.2 add_bitcast_fusion.2
  349.2 7.8 fusion.122
  357.0 9.2 add_bitcast_fusion.2
  382.9 6.3 subtract_bitcast_fusion.2
  390.8 7.8 fusion.122
  398.6 9.2 add_bitcast_fusion.2
  432.5 7.8 fusion.122
  440.3 9.2 add_bitcast_fusion.2
  474.1 7.8 fusion.122
  482.0 9.2 add_bitcast_fusion.2
  515.8 7.8 fusion.122
  523.6 9.2 add_bitcast_fusion.2
  557.5 7.8 fusion.122
  565.3 9.2 add_bitcast_fusion.2
  599.2 7.8 fusion.122
  607.0 9.2 add_bitcast_fusion.2
  640.8 7.8 fusion.122
  648.6 9.2 add_bitcast_fusion.2
  682.5 7.8 fusion.122
  690.3 9.2 add_bitcast_fusion.2
  724.1 7.8 fusion.122
  732.0 9.2 add_bitcast_fusion.2
  765.8 7.8 fusion.122
  773.6 9.2 add_bitcast_fusion.2
  807.5 7.8 fusion.122
  815.3 9.2 add_bitcast_fusion.2
  849.2 7.8 fusion.122
  857.0 9.2 add_bitcast_fusion.2
  890.9 7.8 fusion.122
  898.7 9.2 add_bitcast_fusion.2
  912.4 8.4 add_convert_fusion
  924.6 13.7 copy.29
  938.3 18.8 %reshape.127 = bf16[8,2,65536]{2,1,0:T(2,128)(2,1)S(1)} reshape(bf16[4096,2,8,16]{3,2,1,0:T(8,128)(2,1)} %bitcast.104) | data formatting | bytes 4194304
  957.2 31.7 %all_to_all.36 = bf16[8,2,65536]{2,1,0:T(2,128)(2,1)} all-to-all(bf16[8,2,65536]{2,1,0:T(2,128)(2,1)S(1)} %reshape.127), channel_id=1, replica_groups=mesh['tm'=8,'chan'=4] {'tm'}, dimensions={0} | all-to-all | bytes 4194304 | tf_op jit(solution)/shard_map/all_to_all | solution.py:120
  988.8 13.9 reshape.128
  1002.8 17.5 %copy.31 = bf16[2,16,8,8,512]{4,3,2,1,0:T(8,128)(2,1)S(1)} copy(bf16[2,16,8,8,512]{1,3,0,4,2:T(8,128)(2,1)} %bitcast.105) | data formatting | bytes 4194304 | tf_op jit(solution)/shard_map/all_to_all | solution.py:120
  1025.2 15.3 %pad_maximum_fusion = bf16[2,128,8,4096]{3,2,1,0:T(8,128)(2,1)} fusion(bf16[1,144,8,4096]{3,2,1,0:T(8,128)(2,1)} %bitcast.108, bf16[1,144,8,4096]{3,2,1,0:T(8,128)(2,1)} %copy-done.2), kind=kLoop, calls=%fused_computation.85 | loop fusion | flops 8388608 | bytes 35651584 | tf_op jit(solution)/shard_map/stack | solution.py:114
  1040.5 24.3 %copy.33 = bf16[2,128,8,4096]{1,2,0,3:T(8,128)(2,1)} copy(bf16[2,128,8,4096]{3,2,1,0:T(8,128)(2,1)} %pad_maximum_fusion) | data formatting | bytes 33554432 | tf_op jit(solution)/shard_map/slice | solution.py:116
  1070.7 240.2 %all-gather.2.cloned.1.call-done = bf16[2,64,63,512]{2,1,3,0:T(8,128)(2,1)} async-done(((bf16[2,16,63,512]{2,1,3,0:T(8,128)(2,1)}), bf16[2,64,63,512]{2,1,3,0:T(8,128)(2,1)}) %all-gather.2.cloned.1.call-update) | async-done | bytes 8257552 | tf_op jit(solution)/shard_map/all_gather | solution.py:128
  1311.0 8.3 multiply_reduce_fusion
  1321.7 7.2 slice_bitcast_fusion.1
  1328.9 25.1 %copy.35 = bf16[2,128,8,8,512]{4,3,2,1,0:T(8,128)(2,1)} copy(bf16[2,128,8,8,512]{1,3,0,4,2:T(8,128)(2,1)} %bitcast.20) | data formatting | bytes 33554432 | tf_op jit(solution)/shard_map/all_to_all | solution.py:119
  1354.1 7.5 multiply_reduce_fusion.1
  1371.0 26.8 %copy.44 = bf16[1,128,63,512]{2,1,3,0:T(8,128)(2,1)} copy(bf16[1,128,63,512]{3,2,1,0:T(8,128)(2,1)} %get-tuple-element.101) | data formatting | bytes 16515072
  1397.8 14.2 bitcast_negate_fusion
  1412.0 26.7 %copy.45 = bf16[1,128,63,512]{2,1,3,0:T(8,128)(2,1)} copy(bf16[1,128,63,512]{3,2,1,0:T(8,128)(2,1)} %get-tuple-element.102) | data formatting | bytes 16515072
  1438.6 26.9 %fusion.74 = f32[512,64,128]{2,1,0:T(8,128)} fusion(bf16[128,63,512]{1,0,2:T(8,128)(2,1)} %bitcast.106, bf16[128,63,512]{1,0,2:T(8,128)(2,1)} %bitcast.101, bf16[64,63,512]{1,0,2:T(8,128)(2,1)} %get-tuple-element.100, bf16[64,63,512]{1,0,2:T(8,128)(2,1)} %get-tuple-element.99), kind=kOutput, calls=%fused_computation.86 | convolution fusion | flops 1106509824 | bytes 41549824 | tf_op jit(solution)/shard_map/csf,wsf->cwf/dot_general | solution.py:77
  1465.5 29.8 %bitcast_divide_fusion = f32[128,64,512]{0,1,2:T(8,128)} fusion(f32[512,64,128]{2,1,0:T(8,128)} %fusion.74, bf16[128,63,512]{1,0,2:T(8,128)(2,1)} %bitcast_negate_fusion, bf16[128,63,512]{1,0,2:T(8,128)(2,1)} %bitcast.107, f32[64,512]{0,1:T(8,128)S(1)} %broadcast_add_fusion, f32[128,512]{0,1:T(8,128)S(1)} %copy.38, ...), kind=kOutput, calls=%fused_computation.94 | convolution fusion | flops 1127481344 | bytes 58720256 | tf_op jit(solution)/shard_map/csf,wsf->cwf/dot_general | solution.py:80
  1495.4 17.5 %copy.39 = f32[128,64,512]{2,1,0:T(8,128)} copy(f32[128,64,512]{0,1,2:T(8,128)} %bitcast_divide_fusion) | data formatting | bytes 33554432 | tf_op jit(solution)/shard_map/div | solution.py:85
  (300 shorter events, 462.5 us)
Async XLA Ops:
  6.5 1304.4 %all-gather.2.cloned.1.call-start = ((), (), s32[]{:S(2)}) async-start(), calls=%async_computation.2 | async-start | bytes 20971520 | tf_op jit(solution)/shard_map/all_gather | solution.py:128
  9.6 8.0 copy-start.6
  9.7 38.2 %collective-permute-start = (f32[128,4096]{1,0:T(8,128)}, f32[128,4096]{1,0:T(8,128)}, u32[]{:S(2)}, u32[]{:S(2)}) collective-permute-start(f32[128,4096]{1,0:T(8,128)} %slice.40), channel_id=1, source_target_pairs={{4,0},{8,4},{12,8},{16,12},{20,16},{24,20},{28,24},{5,1},{9,5},{13... | collective-permute-start | bytes 6291464 | tf_op jit(solution)/shard_map/ppermute | solution.py:17
  18.1 29.8 %collective-permute-start.1 = (f32[16,4096]{1,0:T(8,128)S(1)}, f32[16,4096]{1,0:T(8,128)S(1)}, u32[]{:S(2)}, u32[]{:S(2)}) collective-permute-start(f32[16,4096]{1,0:T(8,128)S(1)} %slice.41), channel_id=1, source_target_pairs={{4,0},{8,4},{12,8},{16,12},{20,16},{24,20},{28,24},{5,1},{9,5},{13... | collective-permute-start | bytes 786440 | tf_op jit(solution)/shard_map/ppermute | solution.py:17
  168.5 6.2 copy-start
  182.6 19.2 %copy-start.4 = (bf16[1,64,4096]{2,1,0:T(8,128)(2,1)S(1)}, bf16[1,64,4096]{2,1,0:T(8,128)(2,1)}, u32[]{:S(2)}) copy-start(bf16[1,64,4096]{2,1,0:T(8,128)(2,1)} %broadcast_in_dim.51) | copy-start | bytes 1572868 | tf_op jit(solution)/shard_map/while
  210.1 6.2 copy-start
  224.2 19.2 %copy-start.4 = (bf16[1,64,4096]{2,1,0:T(8,128)(2,1)S(1)}, bf16[1,64,4096]{2,1,0:T(8,128)(2,1)}, u32[]{:S(2)}) copy-start(bf16[1,64,4096]{2,1,0:T(8,128)(2,1)} %broadcast_in_dim.51) | copy-start | bytes 1572868 | tf_op jit(solution)/shard_map/while
  251.7 6.2 copy-start
  265.8 19.2 %copy-start.4 = (bf16[1,64,4096]{2,1,0:T(8,128)(2,1)S(1)}, bf16[1,64,4096]{2,1,0:T(8,128)(2,1)}, u32[]{:S(2)}) copy-start(bf16[1,64,4096]{2,1,0:T(8,128)(2,1)} %broadcast_in_dim.51) | copy-start | bytes 1572868 | tf_op jit(solution)/shard_map/while
  293.4 6.2 copy-start
  307.5 19.2 %copy-start.4 = (bf16[1,64,4096]{2,1,0:T(8,128)(2,1)S(1)}, bf16[1,64,4096]{2,1,0:T(8,128)(2,1)}, u32[]{:S(2)}) copy-start(bf16[1,64,4096]{2,1,0:T(8,128)(2,1)} %broadcast_in_dim.51) | copy-start | bytes 1572868 | tf_op jit(solution)/shard_map/while
  335.1 6.2 copy-start
  349.2 19.2 %copy-start.4 = (bf16[1,64,4096]{2,1,0:T(8,128)(2,1)S(1)}, bf16[1,64,4096]{2,1,0:T(8,128)(2,1)}, u32[]{:S(2)}) copy-start(bf16[1,64,4096]{2,1,0:T(8,128)(2,1)} %broadcast_in_dim.51) | copy-start | bytes 1572868 | tf_op jit(solution)/shard_map/while
  376.7 6.2 copy-start
  390.8 19.2 %copy-start.4 = (bf16[1,64,4096]{2,1,0:T(8,128)(2,1)S(1)}, bf16[1,64,4096]{2,1,0:T(8,128)(2,1)}, u32[]{:S(2)}) copy-start(bf16[1,64,4096]{2,1,0:T(8,128)(2,1)} %broadcast_in_dim.51) | copy-start | bytes 1572868 | tf_op jit(solution)/shard_map/while
  418.4 6.2 copy-start
  432.5 19.2 %copy-start.4 = (bf16[1,64,4096]{2,1,0:T(8,128)(2,1)S(1)}, bf16[1,64,4096]{2,1,0:T(8,128)(2,1)}, u32[]{:S(2)}) copy-start(bf16[1,64,4096]{2,1,0:T(8,128)(2,1)} %broadcast_in_dim.51) | copy-start | bytes 1572868 | tf_op jit(solution)/shard_map/while
  460.0 6.2 copy-start
  474.1 19.2 %copy-start.4 = (bf16[1,64,4096]{2,1,0:T(8,128)(2,1)S(1)}, bf16[1,64,4096]{2,1,0:T(8,128)(2,1)}, u32[]{:S(2)}) copy-start(bf16[1,64,4096]{2,1,0:T(8,128)(2,1)} %broadcast_in_dim.51) | copy-start | bytes 1572868 | tf_op jit(solution)/shard_map/while
  501.7 6.2 copy-start
  515.8 19.2 %copy-start.4 = (bf16[1,64,4096]{2,1,0:T(8,128)(2,1)S(1)}, bf16[1,64,4096]{2,1,0:T(8,128)(2,1)}, u32[]{:S(2)}) copy-start(bf16[1,64,4096]{2,1,0:T(8,128)(2,1)} %broadcast_in_dim.51) | copy-start | bytes 1572868 | tf_op jit(solution)/shard_map/while
  543.4 6.2 copy-start
  557.5 19.2 %copy-start.4 = (bf16[1,64,4096]{2,1,0:T(8,128)(2,1)S(1)}, bf16[1,64,4096]{2,1,0:T(8,128)(2,1)}, u32[]{:S(2)}) copy-start(bf16[1,64,4096]{2,1,0:T(8,128)(2,1)} %broadcast_in_dim.51) | copy-start | bytes 1572868 | tf_op jit(solution)/shard_map/while
  585.1 6.2 copy-start
  599.2 19.2 %copy-start.4 = (bf16[1,64,4096]{2,1,0:T(8,128)(2,1)S(1)}, bf16[1,64,4096]{2,1,0:T(8,128)(2,1)}, u32[]{:S(2)}) copy-start(bf16[1,64,4096]{2,1,0:T(8,128)(2,1)} %broadcast_in_dim.51) | copy-start | bytes 1572868 | tf_op jit(solution)/shard_map/while
  626.7 6.2 copy-start
  640.8 19.2 %copy-start.4 = (bf16[1,64,4096]{2,1,0:T(8,128)(2,1)S(1)}, bf16[1,64,4096]{2,1,0:T(8,128)(2,1)}, u32[]{:S(2)}) copy-start(bf16[1,64,4096]{2,1,0:T(8,128)(2,1)} %broadcast_in_dim.51) | copy-start | bytes 1572868 | tf_op jit(solution)/shard_map/while
  668.4 6.2 copy-start
  682.5 19.2 %copy-start.4 = (bf16[1,64,4096]{2,1,0:T(8,128)(2,1)S(1)}, bf16[1,64,4096]{2,1,0:T(8,128)(2,1)}, u32[]{:S(2)}) copy-start(bf16[1,64,4096]{2,1,0:T(8,128)(2,1)} %broadcast_in_dim.51) | copy-start | bytes 1572868 | tf_op jit(solution)/shard_map/while
  710.1 6.2 copy-start
  724.1 19.2 %copy-start.4 = (bf16[1,64,4096]{2,1,0:T(8,128)(2,1)S(1)}, bf16[1,64,4096]{2,1,0:T(8,128)(2,1)}, u32[]{:S(2)}) copy-start(bf16[1,64,4096]{2,1,0:T(8,128)(2,1)} %broadcast_in_dim.51) | copy-start | bytes 1572868 | tf_op jit(solution)/shard_map/while
  751.7 6.2 copy-start
  765.8 19.2 %copy-start.4 = (bf16[1,64,4096]{2,1,0:T(8,128)(2,1)S(1)}, bf16[1,64,4096]{2,1,0:T(8,128)(2,1)}, u32[]{:S(2)}) copy-start(bf16[1,64,4096]{2,1,0:T(8,128)(2,1)} %broadcast_in_dim.51) | copy-start | bytes 1572868 | tf_op jit(solution)/shard_map/while
  793.4 6.2 copy-start
  807.5 19.2 %copy-start.4 = (bf16[1,64,4096]{2,1,0:T(8,128)(2,1)S(1)}, bf16[1,64,4096]{2,1,0:T(8,128)(2,1)}, u32[]{:S(2)}) copy-start(bf16[1,64,4096]{2,1,0:T(8,128)(2,1)} %broadcast_in_dim.51) | copy-start | bytes 1572868 | tf_op jit(solution)/shard_map/while
  835.1 6.2 copy-start
  849.2 19.2 %copy-start.4 = (bf16[1,64,4096]{2,1,0:T(8,128)(2,1)S(1)}, bf16[1,64,4096]{2,1,0:T(8,128)(2,1)}, u32[]{:S(2)}) copy-start(bf16[1,64,4096]{2,1,0:T(8,128)(2,1)} %broadcast_in_dim.51) | copy-start | bytes 1572868 | tf_op jit(solution)/shard_map/while
  876.8 6.2 copy-start
  890.9 19.2 %copy-start.4 = (bf16[1,64,4096]{2,1,0:T(8,128)(2,1)S(1)}, bf16[1,64,4096]{2,1,0:T(8,128)(2,1)}, u32[]{:S(2)}) copy-start(bf16[1,64,4096]{2,1,0:T(8,128)(2,1)} %broadcast_in_dim.51) | copy-start | bytes 1572868 | tf_op jit(solution)/shard_map/while
  912.4 12.0 copy-start.5
  920.8 3.6 copy-start.2
  1064.8 264.1 %all-to-all-start.1 = ((bf16[2,128,8,4096]{1,2,0,3:T(8,128)(2,1)}), bf16[2,128,8,4096]{1,2,0,3:T(8,128)(2,1)}, u32[]{:S(2)}, u32[]{:S(2)}) async-start(bf16[2,128,8,4096]{1,2,0,3:T(8,128)(2,1)} %copy.33), calls=%async_computation.1 | async-start | bytes 33554432 | tf_op jit(solution)/shard_map/all_to_all | solution.py:119
  1311.0 10.7 copy-start.3
  1354.1 10.7 copy-start.1
Sparse Core Ops, SparseCore 0:
  1025.3 285.5 all-gather.1
where the time goes:
time: 1530 us; the launch traced here: 1520 us
  matrix products  663 us (43%)
  local copies, waits for them, and re-layouts  411 us (27%)
  waiting for transfers between devices  240 us (16%)
  other arithmetic  108 us (7%)
  blocking collectives  59.9 us (4%)
  loops' own time  15.9 us (1%)
    all_gather x1, waiting for transfers between devices, per_device(): lax.all_gather(wit_moved, 'chan', axis=1, tiled=True)  240 us
    dot_general x18, matrix products, transform_block(): jnp.einsum('rkq,qm->rmk', real_two, cos_second, precision=highest)  166 us
    dot_general x18, matrix products, transform_block(): jnp.einsum('rkq,qm->rmk', imag_two, sin_second, precision=highest)  141 us
    dot_general x18, matrix products, transform_block(): jnp.einsum('rkq,qm->rmk', real_two, sin_second, precision=highest)  113 us
    dot_general x18, matrix products, transform_block(): jnp.einsum('rkq,qm->rmk', imag_two, cos_second, precision=highest)  112 us
    unnamed x15, local copies, waits for them, and re-layouts  100 us
    broadcast_in_dim x36, local copies, waits for them, and re-layouts, transform(): real_out, imag_out = lax.map(transform_block, blocks)  67.4 us
    while x108, local copies, waits for them, and re-layouts  38.3 us
  transfers between devices with their start and end apart: 4, of which 1 were waited for; matrix products, arithmetic and copies ran while one was open for 4% of the time, Pallas kernels for 0%

commit v1 on v0

v1 whole, which is shorter than its diff:
```python
import functools
import math

import jax
import jax.numpy as jnp
import numpy as np
from jax import lax
from jax.experimental import pallas as pl
from jax.experimental.pallas import tpu as pltpu
from jax.sharding import PartitionSpec as P

SEG_LEN = 8192
STRIDE = 4096
BINS = 4096
LANES = 128
ROWS = SEG_LEN // LANES
HALF = STRIDE // LANES
INNER = SEG_LEN // LANES
MS = BINS // LANES


def split_high_low(value):
    high = value.astype(jnp.bfloat16)
    low = (value - high.astype(jnp.float32)).astype(jnp.bfloat16)
    return high, low


def tables():
    position = np.arange(SEG_LEN, dtype=np.float64)
    window = (0.5 - 0.5 * np.cos(2.0 * np.pi * position / SEG_LEN)).reshape(ROWS, LANES)
    k1 = np.arange(LANES)
    first = np.zeros((2, 2, ROWS, 2, 2, LANES))
    for half in range(2):
        p = 2 * np.arange(ROWS) + half
        angle = 2.0 * np.pi * (np.outer(p, k1) % LANES) / LANES
        for pair in range(2):
            first[half, pair, :, pair, 0] = np.cos(angle)
            first[half, pair, :, pair, 1] = -np.sin(angle)
    first = first.reshape(4 * ROWS, 4 * LANES)
    q = np.arange(INNER)
    twist = 2.0 * np.pi * np.outer(q, k1) / SEG_LEN
    m = np.arange(MS)
    angle = 2.0 * np.pi * (np.outer(m, q) % INNER) / INNER
    cos, sin = np.cos(angle), np.sin(angle)
    second = np.block([[cos, sin], [-sin, cos]])
    first = jnp.asarray(first, jnp.float32)
    second = jnp.asarray(second, jnp.float32)
    first_high, first_low = split_high_low(first)
    second_high, second_low = split_high_low(second)
    stacked = jnp.concatenate(
        [
            jnp.concatenate([second_high, second_high], axis=1),
            jnp.concatenate([second_low, jnp.zeros_like(second_low)], axis=1),
        ],
        axis=0,
    )
    return (
        jnp.asarray(window, jnp.float32),
        first_high,
        first_low,
        jnp.asarray(np.cos(twist), jnp.float32),
        jnp.asarray(np.sin(twist), jnp.float32),
        stacked,
    )


def transform_kernel(
    seg_count, dests, x_ref, halo_ref, corr_ref, keep_ref, window_ref, fh_ref, fl_ref,
    cos_ref, sin_ref, g_ref, out_ref
):
    per = MS // dests

    def one_channel(c, carry):
        window = window_ref[...]
        cos, sin = cos_ref[...], sin_ref[...]
        blocks = [x_ref[c, pl.ds(HALF * s, HALF), :] for s in range(seg_count)]
        blocks.append(halo_ref[c])
        lefts = []
        for pair in range(seg_count // 2):
            s = 2 * pair
            stacked = jnp.concatenate(
                [
                    jnp.concatenate([blocks[s], blocks[s + 1]], axis=0) * window,
                    jnp.concatenate([blocks[s + 1], blocks[s + 2]], axis=0) * window,
                ],
                axis=0,
            )
            turned = stacked.T
            lefts.append(jnp.concatenate([turned[:INNER], turned[INNER:]], axis=1))
        left = jnp.concatenate(lefts, axis=0)
        high, low = split_high_low(left)
        fh = fh_ref[...]
        y = (
            jnp.dot(high, fh, preferred_element_type=jnp.float32)
            + jnp.dot(low, fh, preferred_element_type=jnp.float32)
            + jnp.dot(high, fl_ref[...], preferred_element_type=jnp.float32)
        )
        for pair in range(seg_count // 2):
            yy = y[INNER * pair : INNER * (pair + 1)]
            columns = []
            for j in range(2):
                re = yy[:, (2 * j) * LANES : (2 * j + 1) * LANES]
                im = yy[:, (2 * j + 1) * LANES : (2 * j + 2) * LANES]
                turned = jnp.concatenate([re * cos + im * sin, im * cos - re * sin], axis=0)
                columns.append(turned)
            both = jnp.concatenate(columns, axis=1)
            bh, bl = split_high_low(both)
            z = jnp.dot(
                g_ref[...], jnp.concatenate([bh, bl], axis=0), preferred_element_type=jnp.float32
            )
            z = z[: 2 * MS] + z[2 * MS :]
            for j in range(2):
                s = 2 * pair + j
                keep = keep_ref[pl.ds(s, 1), :]
                zs = z[:, j * LANES : (j + 1) * LANES]
                real = jnp.concatenate([zs[:8] + corr_ref[c], zs[8:MS]], axis=0)
                real = (real * keep).astype(jnp.bfloat16)
                imag = (zs[MS:] * keep).astype(jnp.bfloat16)
                for d in range(dests):
                    out_ref[d, 0, c, s] = real[per * d : per * (d + 1)]
                    out_ref[d, 1, c, s] = imag[per * d : per * (d + 1)]
        return carry

    lax.fori_loop(0, x_ref.shape[0], one_channel, 0)


def transform(series, halo, corr, keep, tabs, dests):
    channels = series.shape[0]
    seg_count = series.shape[1] // HALF
    block = math.gcd(channels, 8)
    per = MS // dests
    whole = lambda a: pl.BlockSpec(a.shape, lambda i: (0,) * a.ndim)
    return pl.pallas_call(
        functools.partial(transform_kernel, seg_count, dests),
        grid=(channels // block,),
        in_specs=[
            pl.BlockSpec((block,) + series.shape[1:], lambda i: (i, 0, 0)),
            pl.BlockSpec((block,) + halo.shape[1:], lambda i: (i, 0, 0)),
            pl.BlockSpec((block,) + corr.shape[1:], lambda i: (i, 0, 0)),
            whole(keep),
        ]
        + [whole(a) for a in tabs],
        out_specs=pl.BlockSpec(
            (dests, 2, block, seg_count, per, LANES), lambda i: (0, 0, i, 0, 0, 0)
        ),
        out_shape=jax.ShapeDtypeStruct(
            (dests, 2, channels, seg_count, per, LANES), jnp.bfloat16
        ),
        compiler_params=pltpu.CompilerParams(
            dimension_semantics=("arbitrary",), vmem_limit_bytes=48 * 1024 * 1024
        ),
    )(series, halo, corr, keep, *tabs)


def shifted(value, axis, by):
    peers = lax.axis_size(axis)
    pairs = [(i, i + by) for i in range(peers) if 0 <= i + by < peers]
    return lax.ppermute(value, axis, pairs)


def gather_channels(piece, axis):
    peers = lax.axis_size(axis)
    me = lax.axis_index(axis)
    rows = piece.shape[1]
    whole = jnp.zeros((piece.shape[0], rows * peers) + piece.shape[2:], piece.dtype)
    whole = lax.dynamic_update_slice_in_dim(whole, piece, me * rows, 1)
    for step in range(1, peers):
        moved = lax.ppermute(piece, axis, [(i, (i + step) % peers) for i in range(peers)])
        owner = lax.rem(me - step + peers, peers)
        whole = lax.dynamic_update_slice_in_dim(whole, moved, owner * rows, 1)
    return whole


def exchange(spectra):
    moved = lax.all_to_all(spectra, "tm", split_axis=0, concat_axis=0, tiled=True)
    moved = moved.transpose(1, 2, 0, 3, 4, 5)
    parts, channels, sources, segs, per, lanes = moved.shape
    return moved.reshape(parts, channels, sources * segs, per * lanes)


def per_device(auxiliary, proofs):
    aux_rows = auxiliary.shape[0]
    wit_rows = proofs.shape[0]
    tm_size = lax.axis_size("tm")
    seg_count = auxiliary.shape[1] // STRIDE
    tabs = tables()
    wit_series = proofs.reshape(wit_rows, -1, LANES)
    aux_series = auxiliary.reshape(aux_rows, -1, LANES)
    next_wit = shifted(proofs[:, :STRIDE], "tm", -1).reshape(wit_rows, HALF, LANES)
    next_aux = shifted(auxiliary[:, :STRIDE], "tm", -1).reshape(aux_rows, HALF, LANES)
    sums = jnp.concatenate([jnp.sum(proofs, axis=1), jnp.sum(auxiliary, axis=1)])
    totals = jnp.sum(lax.all_gather(sums, "tm"), axis=0)
    means = totals / (auxiliary.shape[1] * tm_size)
    place = np.zeros((8, LANES), np.float32)
    place[0, 0] = -0.5 * SEG_LEN
    place[0, 1] = 0.25 * SEG_LEN
    corr = means[:, None, None] * place[None]
    last = lax.axis_index("tm") == tm_size - 1
    seg_index = jnp.arange(seg_count)[:, None] + jnp.zeros((1, LANES), jnp.int32)
    keep = jnp.where(last & (seg_index == seg_count - 1), 0.0, 1.0).astype(jnp.float32)
    wit_spec = transform(wit_series, next_wit, corr[:wit_rows], keep, tabs, tm_size)
    wit = gather_channels(exchange(wit_spec), "chan")
    aux_spec = transform(aux_series, next_aux, corr[wit_rows:], keep, tabs, tm_size)
    aux = exchange(aux_spec)
    aux_float = aux.astype(jnp.float32)
    aux_power = jnp.sum(aux_float * aux_float, axis=(0, 2))
    wit_float = wit.astype(jnp.float32)
    wit_power = jnp.sum(wit_float * wit_float, axis=(0, 2))
    left_real = jnp.concatenate([aux[0], aux[1]], axis=1)
    left_imag = jnp.concatenate([aux[1], -aux[0]], axis=1)
    right_side = jnp.concatenate([wit[0], wit[1]], axis=1)
    cross_real = jnp.einsum(
        "csf,wsf->cwf", left_real, right_side, preferred_element_type=jnp.float32
    )
    cross_imag = jnp.einsum(
        "csf,wsf->cwf", left_imag, right_side, preferred_element_type=jnp.float32
    )
    return (cross_real * cross_real + cross_imag * cross_imag) / (
        (aux_power[:, None, :] + 1e-06) * (wit_power[None, :, :] + 1e-06)
    )


def solution(mesh):
    return jax.shard_map(
        per_device,
        mesh=mesh,
        in_specs=(P("chan", "tm"), P("chan", "tm")),
        out_specs=P("chan", None, "tm"),
        check_vma=False,
    )
```

time: 1530 us -> 611 us (0.40)
  matrix products: 663 us -> 53 us
  local copies, waits for them, and re-layouts: 411 us -> 206 us
  Pallas kernels: 0 us -> 97.2 us
  waiting for transfers between devices: 240 us -> 159 us
  other arithmetic: 108 us -> 47.3 us
  blocking collectives: 59.9 us -> 26.8 us
  loops' own time: 15.9 us -> 0 us
    dot_general x110 -> x2, matrix products: 663 us -> 53 us  [the longest x1 28.5 us: per_device(): jnp.einsum('csf,wsf->cwf', left_real, right_side, preferred_element_type=...]
    all_gather x1 -> x0, waiting for transfers between devices: 240 us -> none  [per_device(): lax.all_gather(wit_moved, 'chan', axis=1, tiled=True)]
    ppermute x0 -> x3, waiting for transfers between devices: none -> 159 us  [gather_channels(): lax.ppermute(piece, axis, [(i, (i + step) % peers) for i in range(peers)])]
    pallas_call x0 -> x2, Pallas kernels: none -> 97.2 us  [transform(): pl.pallas_call(functools.partial(transform_kernel, seg_count, dests), gri...]
    unnamed x15 -> x30, local copies, waits for them, and re-layouts: 100 us -> 19.9 us
    squeeze x1 -> x4, local copies, waits for them, and re-layouts: 7.24 us -> 76.5 us  [the longest x3 63.8 us: per_device(): left_real = jnp.concatenate([aux[0], aux[1]], axis=1)]
    broadcast_in_dim x36 -> x1, local copies, waits for them, and re-layouts: 67.4 us -> 6.59 us  [gather_channels(): jnp.zeros((piece.shape[0], rows * peers) + piece.shape[2:], piece.dtype)]
    slice x4 -> x3, local copies, waits for them, and re-layouts: 76.6 us -> 15.7 us  [the longest x1 15.7 us: per_device(): left_real = jnp.concatenate([aux[0], aux[1]], axis=1)]
  transfers between devices with their start and end apart: 4 -> 7, of which waited for: 1 -> 2; matrix products, arithmetic and copies ran while one was open for 4% -> 16% of each run, Pallas kernels for 0% -> 16%
where the time goes in v1:
time: 611 us; the launch traced here: 608 us
  local copies, waits for them, and re-layouts  206 us (34%)
  waiting for transfers between devices  159 us (26%)
  Pallas kernels  97.2 us (16%)
  matrix products  53 us (9%)
  other arithmetic  47.3 us (8%)
  blocking collectives  26.8 us (4%)
  starting transfers between devices  18.2 us (3%)
    ppermute x3, waiting for transfers between devices, gather_channels(): lax.ppermute(piece, axis, [(i, (i + step) % peers) for i in range(peers)])  159 us
    pallas_call x2, Pallas kernels, transform(): pl.pallas_call(functools.partial(transform_kernel, seg_count, dests), gri...  97.2 us
    squeeze x3, local copies, waits for them, and re-layouts, per_device(): left_real = jnp.concatenate([aux[0], aux[1]], axis=1)  63.8 us
    dot_general x1, matrix products, per_device(): jnp.einsum('csf,wsf->cwf', left_real, right_side, preferred_element_type=...  28.5 us
    unnamed x1, blocking collectives  26.8 us
    dot_general x1, matrix products, per_device(): jnp.einsum('csf,wsf->cwf', left_imag, right_side, preferred_element_type=...  24.4 us
    concatenate x1, local copies, waits for them, and re-layouts, per_device(): left_imag = jnp.concatenate([aux[1], -aux[0]], axis=1)  23.7 us
    unnamed x30, local copies, waits for them, and re-layouts  19.9 us
  transfers between devices with their start and end apart: 7, of which 2 were waited for; matrix products, arithmetic and copies ran while one was open for 16% of the time, Pallas kernels for 16%

profile of v1, /device:TPU:0, one launch (start us, length us, event | category | flops | bytes accessed | tf_op | source)
XLA Modules:
  0.0 608.3 jit_solution(9712971203672122542)
XLA Ops:
  0.0 0.0 copy-start.3
  0.0 0.0 copy-start.4
  0.0 0.0 copy-start.5
  0.1 0.0 copy-start.8
  0.1 1.8 slice.28
  1.9 1.3 collective-permute-start
  3.2 3.1 slice.32
  6.3 1.3 collective-permute-start.4
  7.6 6.6 %reduce_sum.46 = f32[128]{0:T(128)S(1)} reduce(f32[128,32768]{1,0:T(8,128)} %param.8, f32[]{:T(128)} %constant.23.clone.1), dimensions={1}, to_apply=%region_1.0 | reduce | flops 4194176 | bytes 16777732 | tf_op jit(solution)/shard_map/reduce_sum | solution.py:191
  14.2 0.0 copy-done.8
  14.2 0.4 reduce_sum.45
  14.6 0.0 copy-done.11
  14.6 0.7 dynamic-slice
  16.0 0.2 maximum_dynamic-update-slice_fusion
  16.2 26.8 %all-reduce.1 = f32[1152]{0:T(1024)S(1)} all-reduce(f32[1152]{0:T(1024)S(1)} %maximum_dynamic-update-slice_fusion), channel_id=2, replica_groups=mesh['tm'=8,'chan'=4] {'tm'}, use_global_device_ids=true, to_apply=%add.1 | all-reduce | flops 1152 | bytes 9216
  43.0 0.1 reshape.42
  43.1 0.0 copy-done.10
  43.1 0.2 broadcast_multiply_fusion
  43.4 2.0 copy.61
  45.4 0.0 collective-permute-done
  45.4 1.0 copy.62
  46.4 0.1 add.68.keep_ref
  46.5 0.0 copy-done.2
  46.5 0.0 copy-done
  46.5 11.5 %shard_map.82 = bf16[8,2,16,8,4,128]{5,4,3,2,1,0:T(4,128)(2,1)} custom-call(f32[16,256,128]{2,1,0:T(8,128)S(1)} %bitcast.30, f32[16,32,128]{2,1,0:T(8,128)S(1)} %bitcast.31, f32[16,8,128]{2,1,0:T(8,128)S(1)} %slice.36.corr_ref, f32[8,128]{1,0:T(8,128)S(1)} %add.68.keep_ref, f32[64,128]{1,0:T(8,128)S(1)} %copy-done.5, bf16[256,512]{1,0:T(8,128)(2,1)S(1)} %copy-done.1, ...), custom_call_target="tpu_custom_call" | custom-call | tf_op jit(solution)/shard_map/pallas_call | solution.py:133
  58.0 5.2 all-to-all-start
  63.2 14.2 %copy.63 = f32[16,8,256,128]{3,2,1,0:T(8,128)} copy(f32[16,8,256,128]{3,1,2,0:T(8,128)} %bitcast.32) | data formatting | bytes 33554432
  77.4 0.0 collective-permute-done.4
  77.4 2.0 copy.64
  79.4 85.6 %shard_map.83 = bf16[8,2,128,8,4,128]{5,4,3,2,1,0:T(4,128)(2,1)} custom-call(f32[128,256,128]{2,1,0:T(8,128)} %bitcast.33, f32[128,32,128]{2,1,0:T(8,128)S(1)} %bitcast.29, f32[128,8,128]{2,1,0:T(8,128)S(1)} %slice.39.corr_ref, f32[8,128]{1,0:T(8,128)S(1)} %add.68.keep_ref, f32[64,128]{1,0:T(8,128)S(1)} %copy-done.5, bf16[256,512]{1,0:T(8,128)(2,1)S(1)} %copy-done.1, ...), custom_call_target="tpu_custom_call" | custom-call | tf_op jit(solution)/shard_map/pallas_call | solution.py:133
  165.0 0.0 all-to-all-done
  165.0 5.8 all-to-all-start.1
  170.8 2.2 copy.70
  173.0 3.7 collective-permute-start.3
  176.6 0.0 collective-permute-start.2
  176.6 1.0 collective-permute-start.1
  177.6 4.8 copy.49
  182.5 6.6 %broadcast_in_dim.16 = bf16[2,64,64,512]{2,1,3,0:T(8,128)(2,1)} broadcast(bf16[]{:T(256)} %constant.22.clone.1), dimensions={} | broadcast | bytes 8388610 | tf_op jit(solution)/shard_map/broadcast_in_dim | solution.py:165
  189.1 2.7 constant_dynamic-update-slice_fusion.3
  191.8 30.9 %collective-permute-done.3 = bf16[2,16,64,512]{3,2,1,0:T(8,128)(2,1)} collective-permute-done((bf16[2,16,64,512]{3,2,1,0:T(8,128)(2,1)S(1)}, bf16[2,16,64,512]{3,2,1,0:T(8,128)(2,1)}, u32[]{:S(2)}, u32[]{:S(2)}) %collective-permute-start.3) | collective-permute-done | bytes 2097184 | tf_op jit(solution)/shard_map/ppermute | solution.py:168
  222.7 6.2 %copy.52 = bf16[2,16,64,512]{2,1,3,0:T(8,128)(2,1)} copy(bf16[2,16,64,512]{3,2,1,0:T(8,128)(2,1)} %collective-permute-done.3) | data formatting | bytes 4194304 | tf_op jit(solution)/shard_map/ppermute | solution.py:168
  229.0 128.0 %collective-permute-done.2 = bf16[2,16,64,512]{3,2,1,0:T(8,128)(2,1)} collective-permute-done((bf16[2,16,64,512]{3,2,1,0:T(8,128)(2,1)S(1)}, bf16[2,16,64,512]{3,2,1,0:T(8,128)(2,1)}, u32[]{:S(2)}, u32[]{:S(2)}) %collective-permute-start.2) | collective-permute-done | bytes 2097184 | tf_op jit(solution)/shard_map/ppermute | solution.py:168
  356.9 6.2 %copy.51 = bf16[2,16,64,512]{2,1,3,0:T(8,128)(2,1)} copy(bf16[2,16,64,512]{3,2,1,0:T(8,128)(2,1)} %collective-permute-done.2) | data formatting | bytes 4194304 | tf_op jit(solution)/shard_map/ppermute | solution.py:168
  363.1 0.0 collective-permute-done.1
  363.1 6.1 %copy.50 = bf16[2,16,64,512]{2,1,3,0:T(8,128)(2,1)} copy(bf16[2,16,64,512]{3,2,1,0:T(8,128)(2,1)} %collective-permute-done.1) | data formatting | bytes 4194304 | tf_op jit(solution)/shard_map/ppermute | solution.py:168
  369.3 5.1 constant_dynamic-update-slice_fusion.2
  374.3 4.9 constant_dynamic-update-slice_fusion.1
  379.3 2.7 constant_dynamic-update-slice_fusion
  382.0 8.0 %multiply_reduce_fusion = f32[64,512]{0,1:T(8,128)S(1)} fusion(bf16[2,64,64,512]{2,1,3,0:T(8,128)(2,1)} %constant_dynamic-update-slice_fusion), kind=kLoop, calls=%fused_computation | loop fusion | flops 12550144 | bytes 8519680 | tf_op jit(solution)/shard_map/reduce_sum | solution.py:208
  390.1 12.7 %slice_bitcast_fusion.1 = (bf16[64,64,512]{1,0,2:T(8,128)(2,1)}, bf16[64,64,512]{1,0,2:T(8,128)(2,1)}) fusion(bf16[2,64,64,512]{2,1,3,0:T(8,128)(2,1)} %constant_dynamic-update-slice_fusion), kind=kLoop, calls=%fused_computation.9 | loop fusion | bytes 16777216 | tf_op jit(solution)/shard_map/squeeze | solution.py:211
  402.8 0.0 all-to-all-done.1
  402.8 10.4 %multiply_reduce_fusion.1 = f32[128,4,128]{2,1,0:T(4,128)S(1)} fusion(bf16[8,2,128,8,4,128]{5,4,3,2,1,0:T(4,128)(2,1)} %all-to-all-done.1), kind=kLoop, calls=%fused_computation.1 | loop fusion | flops 25100288 | bytes 17039360 | tf_op jit(solution)/shard_map/reduce_sum | solution.py:206
  413.1 0.1 broadcast_add_fusion.1
  413.2 0.1 copy.60
  413.3 15.7 %fusion.8 = (bf16[1,128,8,8,4,128]{5,4,3,1,0,2:T(4,128)(2,1)}, bf16[1,128,8,8,4,128]{5,4,3,1,0,2:T(4,128)(2,1)}) fusion(bf16[2,128,8,8,4,128]{5,4,3,1,0,2:T(4,128)(2,1)} %bitcast.5), kind=kLoop, calls=%fused_computation.28 | loop fusion | bytes 33554432 | tf_op jit(solution)/shard_map/slice | solution.py:209
  429.0 7.7 %fusion.7 = bf16[128,64,512]{2,1,0:T(8,128)(2,1)} fusion(bf16[1,128,8,8,4,128]{5,4,3,1,0,2:T(4,128)(2,1)} %get-tuple-element.7), kind=kLoop, calls=%fused_computation.27 | loop fusion | flops 4194304 | bytes 16777216 | tf_op jit(solution)/shard_map/neg | solution.py:210
  436.7 16.0 %copy_bitcast_fusion = (bf16[128,64,512]{2,1,0:T(8,128)(2,1)}, bf16[128,64,512]{2,1,0:T(8,128)(2,1)}) fusion(bf16[1,128,8,8,4,128]{5,4,3,1,0,2:T(4,128)(2,1)} %get-tuple-element.8, bf16[1,128,8,8,4,128]{5,4,3,1,0,2:T(4,128)(2,1)} %get-tuple-element.7), kind=kLoop, calls=%fused_computation.11 | loop fusion | bytes 33554432 | tf_op jit(solution)/shard_map/squeeze | solution.py:209
  452.7 23.9 %copy.55 = bf16[128,64,512]{1,0,2:T(8,128)(2,1)} copy(bf16[128,64,512]{2,1,0:T(8,128)(2,1)} %get-tuple-element.10) | data formatting | bytes 16777216 | tf_op jit(solution)/shard_map/squeeze | solution.py:209
  476.6 23.9 %copy.56 = bf16[128,64,512]{1,0,2:T(8,128)(2,1)} copy(bf16[128,64,512]{2,1,0:T(8,128)(2,1)} %get-tuple-element.9) | data formatting | bytes 16777216 | tf_op jit(solution)/shard_map/squeeze | solution.py:209
  500.6 13.7 %pad_maximum_fusion = bf16[128,128,512]{2,1,0:T(8,128)(2,1)} fusion(bf16[128,64,512]{2,1,0:T(8,128)(2,1)} %fusion.7, bf16[128,64,512]{2,1,0:T(8,128)(2,1)} %get-tuple-element.9), kind=kLoop, calls=%fused_computation.6 | loop fusion | flops 33554432 | bytes 33554432 | tf_op jit(solution)/shard_map/concatenate | solution.py:210
  514.3 23.7 %copy.57 = bf16[128,128,512]{1,0,2:T(8,128)(2,1)} copy(bf16[128,128,512]{2,1,0:T(8,128)(2,1)} %pad_maximum_fusion) | data formatting | bytes 33554432 | tf_op jit(solution)/shard_map/concatenate | solution.py:210
  537.9 28.5 %fusion = f32[512,64,128]{2,1,0:T(8,128)} fusion(bf16[128,64,512]{1,0,2:T(8,128)(2,1)} %copy.56, bf16[128,64,512]{1,0,2:T(8,128)(2,1)} %copy.55, bf16[64,64,512]{1,0,2:T(8,128)(2,1)} %get-tuple-element.6, bf16[64,64,512]{1,0,2:T(8,128)(2,1)} %get-tuple-element.5), kind=kOutput, calls=%fused_computation.2 | convolution fusion | flops 1124073472 | bytes 41943040 | tf_op jit(solution)/shard_map/csf,wsf->cwf/dot_general | solution.py:212
  566.4 24.4 %bitcast_divide_fusion = f32[128,64,512]{0,1,2:T(8,128)} fusion(f32[512,64,128]{2,1,0:T(8,128)} %fusion, f32[64,512]{0,1:T(8,128)S(1)} %broadcast_add_fusion, f32[128,512]{0,1:T(8,128)S(1)} %bitcast.40, bf16[128,128,512]{1,0,2:T(8,128)(2,1)} %copy.57, bf16[64,64,512]{1,0,2:T(8,128)(2,1)} %get-tuple-element.6, bf16[64,64,512]{1,0,2:T(8,128)(2,1)} %get-tuple-element.5), kind=kOutput, calls=%fused_computation.7 | convolution fusion | flops 1111490560 | bytes 59113472 | tf_op jit(solution)/shard_map/csf,wsf->cwf/dot_general | solution.py:215
  590.9 17.5 %copy.59 = f32[128,64,512]{2,1,0:T(8,128)} copy(f32[128,64,512]{0,1,2:T(8,128)} %bitcast_divide_fusion) | data formatting | bytes 33554432 | tf_op jit(solution)/shard_map/div | solution.py:218
  (22 shorter events, 0.1 us)
Async XLA Ops:
  0.0 14.6 %copy-start.11 = (u32[32]{0:T(128)S(1)}, u32[32]{0:T(128)}, u32[]{:S(2)}) copy-start(u32[32]{0:T(128)} %constant.84) | copy-start | bytes 388
  0.0 43.1 %copy-start.10 = (f32[8,128]{1,0:T(8,128)S(1)}, f32[8,128]{1,0:T(8,128)}, u32[]{:S(2)}) copy-start(f32[8,128]{1,0:T(8,128)} %constant.70) | copy-start | bytes 12292
  0.0 46.5 %copy-start.2 = (bf16[128,256]{1,0:T(8,128)(2,1)S(1)}, bf16[128,256]{1,0:T(8,128)(2,1)}, u32[]{:S(2)}) copy-start(bf16[128,256]{1,0:T(8,128)(2,1)} %constant.81.g_ref) | copy-start | bytes 196612
  0.0 46.5 %copy-start = (bf16[256,512]{1,0:T(8,128)(2,1)S(1)}, bf16[256,512]{1,0:T(8,128)(2,1)}, u32[]{:S(2)}) copy-start(bf16[256,512]{1,0:T(8,128)(2,1)} %constant.74.fl_ref) | copy-start | bytes 786436
  0.0 46.5 %copy-start.1 = (bf16[256,512]{1,0:T(8,128)(2,1)S(1)}, bf16[256,512]{1,0:T(8,128)(2,1)}, u32[]{:S(2)}) copy-start(bf16[256,512]{1,0:T(8,128)(2,1)} %constant.71.fh_ref) | copy-start | bytes 786436
  0.0 46.5 %copy-start.3 = (f32[64,128]{1,0:T(8,128)S(1)}, f32[64,128]{1,0:T(8,128)}, u32[]{:S(2)}) copy-start(f32[64,128]{1,0:T(8,128)} %constant.66.clone.sin_ref) | copy-start | bytes 98308
  0.0 46.5 %copy-start.4 = (f32[64,128]{1,0:T(8,128)S(1)}, f32[64,128]{1,0:T(8,128)}, u32[]{:S(2)}) copy-start(f32[64,128]{1,0:T(8,128)} %constant.65.clone.cos_ref) | copy-start | bytes 98308
  0.0 46.5 %copy-start.5 = (f32[64,128]{1,0:T(8,128)S(1)}, f32[64,128]{1,0:T(8,128)}, u32[]{:S(2)}) copy-start(f32[64,128]{1,0:T(8,128)} %constant.64.clone.window_ref) | copy-start | bytes 98308
  0.1 14.1 %copy-start.8 = (f32[16,32768]{1,0:T(8,128)S(1)}, f32[16,32768]{1,0:T(8,128)}, u32[]{:S(2)}) copy-start(f32[16,32768]{1,0:T(8,128)} %param.9) | copy-start | bytes 6291460
  1.9 43.5 %collective-permute-start = (f32[16,4096]{1,0:T(8,128)}, f32[16,4096]{1,0:T(8,128)}, u32[]{:S(2)}, u32[]{:S(2)}) collective-permute-start(f32[16,4096]{1,0:T(8,128)} %slice.28), channel_id=1, source_target_pairs={{4,0},{8,4},{12,8},{16,12},{20,16},{24,20},{28,24},{5,1},{9,5},{13... | collective-permute-start | bytes 786440 | tf_op jit(solution)/shard_map/ppermute | solution.py:158
  6.3 71.1 %collective-permute-start.4 = (f32[128,4096]{1,0:T(8,128)}, f32[128,4096]{1,0:T(8,128)}, u32[]{:S(2)}, u32[]{:S(2)}) collective-permute-start(f32[128,4096]{1,0:T(8,128)} %slice.32), channel_id=1, source_target_pairs={{4,0},{8,4},{12,8},{16,12},{20,16},{24,20},{28,24},{5,1},{9,5},{13... | collective-permute-start | bytes 6291464 | tf_op jit(solution)/shard_map/ppermute | solution.py:158
  58.0 107.0 %all-to-all-start = ((bf16[8,2,16,8,4,128]{5,4,3,2,1,0:T(4,128)(2,1)}), bf16[8,2,16,8,4,128]{5,4,3,2,1,0:T(4,128)(2,1)S(1)}, u32[]{:S(2)}, u32[]{:S(2)}) async-start(bf16[8,2,16,8,4,128]{5,4,3,2,1,0:T(4,128)(2,1)} %shard_map.82), calls=%async_computation | async-start | bytes 4194304 | tf_op jit(solution)/shard_map/all_to_all | solution.py:175
  165.0 5.8 copy-start.9
  165.0 237.7 %all-to-all-start.1 = ((bf16[8,2,128,8,4,128]{5,4,3,2,1,0:T(4,128)(2,1)}), bf16[8,2,128,8,4,128]{5,4,3,2,1,0:T(4,128)(2,1)}, u32[]{:S(2)}, u32[]{:S(2)}) async-start(bf16[8,2,128,8,4,128]{5,4,3,2,1,0:T(4,128)(2,1)} %shard_map.83), calls=%async_computation.1 | async-start | bytes 33554432 | tf_op jit(solution)/shard_map/all_to_all | solution.py:175
  173.0 49.8 %collective-permute-start.3 = (bf16[2,16,64,512]{3,2,1,0:T(8,128)(2,1)S(1)}, bf16[2,16,64,512]{3,2,1,0:T(8,128)(2,1)}, u32[]{:S(2)}, u32[]{:S(2)}) collective-permute-start(bf16[2,16,64,512]{3,2,1,0:T(8,128)(2,1)S(1)} %bitcast.35), channel_id=1, source_target_pairs={{0,3},{1,0},{2,1},{3,2},{4,7},{5,4},{6,5},{7,6},{8,11},{9,8},{10,9... | collective-permute-start | bytes 6291464 | tf_op jit(solution)/shard_map/ppermute | solution.py:168
  176.6 180.3 %collective-permute-start.2 = (bf16[2,16,64,512]{3,2,1,0:T(8,128)(2,1)S(1)}, bf16[2,16,64,512]{3,2,1,0:T(8,128)(2,1)}, u32[]{:S(2)}, u32[]{:S(2)}) collective-permute-start(bf16[2,16,64,512]{3,2,1,0:T(8,128)(2,1)S(1)} %bitcast.36), channel_id=1, source_target_pairs={{0,2},{1,3},{2,0},{3,1},{4,6},{5,7},{6,4},{7,5},{8,10},{9,11},{10,... | collective-permute-start | bytes 6291464 | tf_op jit(solution)/shard_map/ppermute | solution.py:168
  176.6 186.5 %collective-permute-start.1 = (bf16[2,16,64,512]{3,2,1,0:T(8,128)(2,1)S(1)}, bf16[2,16,64,512]{3,2,1,0:T(8,128)(2,1)}, u32[]{:S(2)}, u32[]{:S(2)}) collective-permute-start(bf16[2,16,64,512]{3,2,1,0:T(8,128)(2,1)S(1)} %bitcast.37), channel_id=1, source_target_pairs={{0,1},{1,2},{2,3},{3,0},{4,5},{5,6},{6,7},{7,4},{8,9},{9,10},{10,1... | collective-permute-start | bytes 6291464 | tf_op jit(solution)/shard_map/ppermute | solution.py:168
  182.5 6.6 %copy-start.7 = (bf16[2,16,64,512]{2,1,3,0:T(8,128)(2,1)S(1)}, bf16[2,16,64,512]{2,1,3,0:T(8,128)(2,1)}, u32[]{:S(2)}) copy-start(bf16[2,16,64,512]{2,1,3,0:T(8,128)(2,1)} %copy.49) | copy-start | bytes 6291460
  369.3 10.0 %copy-start.6 = (bf16[2,16,64,512]{2,1,3,0:T(8,128)(2,1)S(1)}, bf16[2,16,64,512]{2,1,3,0:T(8,128)(2,1)}, u32[]{:S(2)}) copy-start(bf16[2,16,64,512]{2,1,3,0:T(8,128)(2,1)} %copy.52) | copy-start | bytes 6291460
